TPU v7x, 32 devices: a whole 2x2x4 slice. The times are simulated.
32 devices in a mesh: group: 2 (over x), frame: 4 (over y, core), row: 4 (over z).
Axes of the slice: x: 2, y: 2, z: 4, core: 2. Of those that a mesh axis runs over, the one named last changes fastest.
Arguments:
- latents: bfloat16 [48, 8, 64, 320], P(('group', 'frame'), 'row'), parts along dimension 0, may hold values from -8 to 8
- condition: bfloat16 [24, 8, 64, 320], P(('group', 'frame'), 'row'), parts along dimension 0, may hold values from -6 to 6
- key_frames: int32 [24], P('group'), parts along dimension 0, may hold values from -1 to 23, as said below
- propagate: int32 [48], P('group'), parts along dimension 0, may hold values from 0 to 11, as said below
- encoder_conv: bfloat16 [9, 320, 320], replicated, may hold values from -0.109375 to 0.109375
- zero_conv: bfloat16 [320, 320], replicated, may hold values from -0.3125 to 0.3125
- attention_gain: float32 [320], replicated, may hold values from 0.25 to 1.75
- query_weight: bfloat16 [320, 320], replicated, may hold values from -3 to 3
- key_weight: bfloat16 [320, 320], replicated, may hold values from -3 to 3
- value_weight: bfloat16 [320, 320], replicated, may hold values from -0.3125 to 0.3125
- output_weight: bfloat16 [320, 320], replicated, may hold values from -0.3125 to 0.3125
- conv_gain: float32 [320], replicated, may hold values from 0.25 to 1.75
- block_conv: bfloat16 [9, 320, 320], replicated, may hold values from -0.109375 to 0.109375
Outputs:
- updated: bfloat16 [48, 8, 64, 320], P(('group', 'frame'), 'row'), parts along dimension 0
There are 2 independent parts, one for each index of `group`. A program takes and returns all parts, laid end to end along the dimension named above; an argument that names none is the same for every part. Nothing has to cross between parts.
Inputs may be any that keep to these rules, and one draw needn't show every extreme that they name: `key_frames`: the 3 slots of index d of frame hold keyframes of frames d * 6 to (d + 1) * 6 - 1, all different, live slots first; of index d and the index half the frame axis away, one holds 3 live keyframes and the other 1. `propagate`: each frame names a live slot of its own index of frame or of an adjacent one (no wrap); a keyframe's own frame names its own slot.
All inputs are finite; a program needn't handle non-finite values.
Results may differ from a plain program's by a relative error of at most 0.014.
Values may be sent and summed in bfloat16 or wider, within the bound.
A program may use at most 64 MiB of HBM per device.

v0:
```python
import functools
import math

import jax
import jax.numpy as jnp
import numpy as np
from jax import lax
from jax.experimental import pallas as pl
from jax.experimental.pallas import tpu as pltpu
from jax.sharding import PartitionSpec as P

HEADS = 8
MESH = pl.DeviceIdType.MESH
F32 = jnp.float32
BF16 = jnp.bfloat16


def positions(frame_total, channels):
    frame_pos = np.arange(frame_total, dtype=np.float64)[:, None]
    half_index = np.arange(channels // 2, dtype=np.float64)
    frequency = np.exp(half_index * (-2.0 * math.log(10000.0) / channels))
    angles = frame_pos * frequency
    stacked = np.stack([np.sin(angles), np.cos(angles)], axis=-1)
    return stacked.reshape(frame_total, channels).astype(np.float32)


def norm(values, gain):
    average = jnp.mean(values, axis=-1, keepdims=True)
    centered = values - average
    variance = jnp.mean(centered * centered, axis=-1, keepdims=True)
    return centered * lax.rsqrt(variance + 1e-05) * gain


def silu(values):
    return values / (1.0 + jnp.exp(-values))


def dot(left, right):
    return jnp.dot(left, right, preferred_element_type=F32)


def flat(values):
    return values.astype(F32).reshape(-1, values.shape[-1]).astype(BF16)


def conv_local(images, weights, sums):
    _, count, rows, cols, channels = sums.shape
    whole = flat(images[...])
    for b in range(3):
        sums[b] = dot(whole, weights[3 + b]).reshape(count, rows, cols, channels)
    if rows > 1:
        upper = flat(images[:, : rows - 1])
        lower = flat(images[:, 1:])
        part = (count, rows - 1, cols, channels)
        for b in range(3):
            sums[b, :, 1:] += dot(upper, weights[b]).reshape(part)
            sums[b, :, : rows - 1] += dot(lower, weights[6 + b]).reshape(part)


def conv_edge(edge, weights, sums, row, taps):
    _, count, _, cols, channels = sums.shape
    values = flat(edge[...])
    for b in range(3):
        sums[b, :, row] += dot(values, weights[taps + b]).reshape(count, cols, channels)


def conv_row(sums, index, row):
    left, middle, right = (sums[b, index, row] for b in range(3))
    cols = middle.shape[0]
    col = lax.broadcasted_iota(jnp.int32, middle.shape, 0)
    left = jnp.where(col == 0, 0.0, pltpu.roll(left, 1, 0))
    right = jnp.where(col == cols - 1, 0.0, pltpu.roll(right, cols - 1, 0))
    return left + middle + right


def kernel(
    n,
    row_total,
    lat,
    cond_hbm,
    key_frames,
    propagate,
    encoding,
    gain_a,
    gain_c,
    enc_hbm,
    zero_hbm,
    q_hbm,
    k_hbm,
    v_hbm,
    o_hbm,
    blk_hbm,
    out_hbm,
    out,
    out_sem,
    cond,
    enc_w,
    zero_w,
    q_w,
    k_w,
    v_w,
    o_w,
    blk_w,
    lat_pix,
    keyres,
    res_pix,
    hidden,
    att_pix,
    att,
    act,
    cond_top,
    cond_bot,
    act_top,
    act_bot,
    sums_e,
    sums_b,
    w_sem,
    own_sem,
    lat_send,
    lat_recv,
    res_send,
    res_recv,
    att_send,
    att_recv,
    ch_send,
    ch_recv,
    ah_send,
    ah_recv,
):
    me = lax.axis_index("frame")
    row_me = lax.axis_index("row")
    frames_dev, _, pix, channels = lat.shape
    slots, rows, cols, _ = cond.shape
    chunks = res_recv.shape[0]
    chunk = pix // chunks
    group = att.shape[3]
    per_chunk = chunk // group
    frames = frames_dev * n
    head_dim = channels // HEADS
    has_up = row_me > 0
    has_down = row_me < row_total - 1

    pairs = [
        (cond_hbm, cond),
        (enc_hbm, enc_w),
        (zero_hbm, zero_w),
        (q_hbm, q_w),
        (k_hbm, k_w),
        (v_hbm, v_w),
        (o_hbm, o_w),
        (blk_hbm, blk_w),
    ]
    loads = [pltpu.make_async_copy(s, d, w_sem.at[i]) for i, (s, d) in enumerate(pairs)]
    for load in loads:
        load.start()

    barrier = pltpu.get_barrier_semaphore()
    for k in range(1, n):
        pl.semaphore_signal(
            barrier, inc=1, device_id={"frame": lax.rem(me + k, n)}, device_id_type=MESH
        )

    @pl.when(has_up)
    def _():
        pl.semaphore_signal(barrier, inc=1, device_id={"row": row_me - 1}, device_id_type=MESH)

    @pl.when(has_down)
    def _():
        pl.semaphore_signal(barrier, inc=1, device_id={"row": row_me + 1}, device_id_type=MESH)

    neighbours = has_up.astype(jnp.int32) + has_down.astype(jnp.int32)
    pl.semaphore_wait(barrier, n - 1 + neighbours)

    def remote(src, dst, send, recv, **where):
        return pltpu.make_async_remote_copy(
            src_ref=src,
            dst_ref=dst,
            send_sem=send,
            recv_sem=recv,
            device_id=where,
            device_id_type=MESH,
        )

    def up(src, dst, send, recv):
        return remote(src, dst, send, recv, row=row_me - 1)

    def down(src, dst, send, recv):
        return remote(src, dst, send, recv, row=row_me + 1)

    cond_up = up(cond_hbm.at[:, 0], cond_bot, ch_send.at[0], ch_recv.at[0])
    cond_down = down(cond_hbm.at[:, rows - 1], cond_top, ch_send.at[1], ch_recv.at[1])
    pl.when(has_up)(cond_up.start)
    pl.when(has_down)(cond_down.start)

    def spread(src, dst, count, send, recv):
        copies = []
        for k in range(1, n):
            peer = lax.rem(me + k, n)
            copies.append(
                remote(
                    src.at[:, peer],
                    dst.at[pl.ds(me * count, count)],
                    send.at[k],
                    recv.at[k],
                    frame=peer,
                )
            )
        return copies

    lat_copies = spread(lat, lat_pix, frames_dev, lat_send, lat_recv)
    for copy in lat_copies:
        copy.start()
    lat_own = pltpu.make_async_copy(
        lat.at[:, me], lat_pix.at[pl.ds(me * frames_dev, frames_dev)], own_sem.at[0]
    )
    lat_own.start()

    @pl.when(jnp.logical_not(has_up))
    def _():
        cond_top[...] = jnp.zeros_like(cond_top)
        act_top[...] = jnp.zeros_like(act_top)

    @pl.when(jnp.logical_not(has_down))
    def _():
        cond_bot[...] = jnp.zeros_like(cond_bot)
        act_bot[...] = jnp.zeros_like(act_bot)

    loads[0].wait()
    loads[1].wait()
    conv_local(cond, enc_w, sums_e)
    pl.when(has_up)(cond_down.wait_recv)
    pl.when(has_down)(cond_up.wait_recv)
    conv_edge(cond_top, enc_w, sums_e, 0, 0)
    conv_edge(cond_bot, enc_w, sums_e, rows - 1, 6)
    loads[2].wait()
    encoded = jnp.concatenate(
        [silu(conv_row(sums_e, s, r)) for s in range(slots) for r in range(rows)], axis=0
    ).astype(BF16)
    keyres[...] = dot(encoded, zero_w[...]).reshape(keyres.shape).astype(BF16)
    res_copies = []
    for c in range(chunks):
        span = pl.ds(c * chunk, chunk)
        for k in range(1, n):
            peer = lax.rem(me + k, n)
            copy = remote(
                keyres.at[:, peer, span],
                res_pix[c].at[pl.ds(me * slots, slots)],
                res_send.at[c, k],
                res_recv.at[c, k],
                frame=peer,
            )
            copy.start()
            res_copies.append(copy)
        own = pltpu.make_async_copy(
            keyres.at[:, me, span], res_pix[c].at[pl.ds(me * slots, slots)], own_sem.at[1 + c]
        )
        own.start()
        res_copies.append(own)

    lat_own.wait()
    for copy in lat_copies:
        copy.wait()

    for load in loads[3:7]:
        load.wait()

    small = frames <= 24
    block = frames * group
    same = lax.rem(lax.broadcasted_iota(jnp.int32, (block, block), 0), group) == lax.rem(
        lax.broadcasted_iota(jnp.int32, (block, block), 1), group
    )
    scale = 1.0 / math.sqrt(head_dim)
    encode = encoding[...][:, None, :]

    def head(h, start, queries, keys, values):
        lane = start + lax.broadcasted_iota(jnp.int32, (1, queries.shape[1]), 1)
        mine = (lane >= h * head_dim) & (lane < (h + 1) * head_dim)
        pick = jnp.where(mine, 1.0, 0.0).astype(BF16)
        scores = lax.dot_general(
            queries * pick, keys, (((1,), (1,)), ((), ())), preferred_element_type=F32
        )
        scores = jnp.where(same, scores * scale, -1e30)
        top = jnp.max(scores, axis=-1, keepdims=True)
        powers = jnp.exp(scores - top)
        probs = (powers / jnp.sum(powers, axis=-1, keepdims=True)).astype(BF16)
        return dot(probs, values * pick)

    def windows(h):
        start = -(-max(0, (h + 1) * head_dim - 256) // 128) * 128
        return start, min(start + 256, channels)

    def attend(queries, keys, values):
        if not small or head_dim > 128:
            return lax.fori_loop(
                0,
                HEADS,
                lambda h, total: total + head(h, 0, queries, keys, values),
                jnp.zeros((block, channels), F32),
            )
        totals = {}
        for h in range(HEADS):
            start, stop = windows(h)
            cut = slice(start, stop)
            mixed = head(h, start, queries[:, cut], keys[:, cut], values[:, cut])
            totals[start] = mixed if start not in totals else totals[start] + mixed
        tiles = []
        for low in range(0, channels, 128):
            high = min(low + 128, channels)
            held = [
                value[:, low - start : high - start]
                for start, value in totals.items()
                if start <= low and high <= start + value.shape[1]
            ]
            tiles.append(sum(held[1:], held[0]))
        return jnp.concatenate(tiles, axis=1)

    att_copies = []
    for c in range(chunks):
        span = slice(c * chunk, (c + 1) * chunk)
        for copy in res_copies[c * n : (c + 1) * n]:
            copy.wait()

        def hide(f, carry):
            slot = propagate[f]
            gap = jnp.abs(f - key_frames[slot]).astype(F32)
            reach = jnp.exp(jnp.full((1, channels), -gap / (2 * frames_dev), F32))
            value = lat_pix[f, span].astype(F32) + reach * res_pix[c][slot].astype(F32)
            hidden[f, span] = value.astype(BF16).astype(F32)
            return carry

        lax.fori_loop(0, frames, hide, 0, unroll=small)
        here = hidden[:, span]
        normed = (norm(here, gain_a[...]) + encode).reshape(-1, channels).astype(BF16)
        full = (frames, chunk, channels)
        query = dot(normed, q_w[...]).reshape(full)
        keyp = dot(normed, k_w[...]).reshape(full)
        valp = dot(normed, v_w[...]).reshape(full)
        for g in range(per_chunk):
            s = c * per_chunk + g
            part = slice(g * group, (g + 1) * group)
            mixed = attend(
                query[:, part].reshape(block, channels).astype(BF16),
                keyp[:, part].reshape(block, channels).astype(BF16),
                valp[:, part].reshape(block, channels).astype(BF16),
            )
            projected = dot(mixed.astype(BF16), o_w[...]).reshape(frames, group, channels)
            base = hidden[:, s * group : (s + 1) * group]
            att_pix[s] = (base + projected).astype(BF16)
            for k in range(1, n):
                peer = lax.rem(me + k, n)
                copy = remote(
                    att_pix.at[s, pl.ds(peer * frames_dev, frames_dev)],
                    att.at[:, me, s],
                    att_send.at[s, k],
                    att_recv.at[s, k],
                    frame=peer,
                )
                copy.start()
                att_copies.append(copy)
            own = pltpu.make_async_copy(
                att_pix.at[s, pl.ds(me * frames_dev, frames_dev)],
                att.at[:, me, s],
                own_sem.at[1 + chunks + s],
            )
            own.start()
            att_copies.append(own)

    pieces = chunks * per_chunk
    piece = (frames_dev, rows, n // rows, group, channels)
    act_ups, act_downs = [], []
    for s in range(pieces):
        for copy in att_copies[s * n : (s + 1) * n]:
            copy.wait()
        value = att[:, :, s].astype(F32)
        act[:, :, :, s] = silu(norm(value, gain_c[...])).astype(BF16).reshape(piece)
        act_up = up(act.at[:, 0, :, s], act_bot.at[:, :, s], ah_send.at[0, s], ah_recv.at[0, s])
        act_down = down(
            act.at[:, rows - 1, :, s], act_top.at[:, :, s], ah_send.at[1, s], ah_recv.at[1, s]
        )
        pl.when(has_up)(act_up.start)
        pl.when(has_down)(act_down.start)
        act_ups.append(act_up)
        act_downs.append(act_down)

    loads[7].wait()
    conv_local(act, blk_w, sums_b)
    for s in range(pieces):
        pl.when(has_up)(act_downs[s].wait_recv)
        pl.when(has_down)(act_ups[s].wait_recv)
    conv_edge(act_top, blk_w, sums_b, 0, 0)
    conv_edge(act_bot, blk_w, sums_b, rows - 1, 6)
    stores = []
    for f in range(frames_dev):
        convolved = jnp.concatenate([conv_row(sums_b, f, r) for r in range(rows)], axis=0)
        value = att[f].astype(F32).reshape(rows * cols, channels)
        out[f] = (value + convolved).reshape(rows, cols, channels).astype(BF16)
        store = pltpu.make_async_copy(out.at[f], out_hbm.at[f], out_sem.at[f])
        store.start()
        stores.append(store)

    pl.when(has_up)(cond_up.wait_send)
    pl.when(has_down)(cond_down.wait_send)
    for store in stores:
        store.wait()
    for s in range(pieces):
        pl.when(has_up)(act_ups[s].wait_send)
        pl.when(has_down)(act_downs[s].wait_send)


def shards(
    latents,
    condition,
    key_frames,
    propagate,
    encoder_conv,
    zero_conv,
    attention_gain,
    query_weight,
    key_weight,
    value_weight,
    output_weight,
    conv_gain,
    block_conv,
):
    frames_dev, rows, cols, channels = latents.shape
    slots = condition.shape[0]
    n = lax.axis_size("frame")
    row_total = lax.axis_size("row")
    pix = rows * cols // n
    frames = frames_dev * n
    chunk = 16 if pix % 16 == 0 else 8
    chunks = pix // chunk
    group = 8
    pieces = pix // group
    per_row = n // rows
    encoding = jnp.asarray(positions(frames, channels))
    square = (channels, channels)
    vmem = pl.BlockSpec(memory_space=pltpu.VMEM)
    smem = pl.BlockSpec(memory_space=pltpu.SMEM)
    anywhere = pl.BlockSpec(memory_space=pl.ANY)
    dma = pltpu.SemaphoreType.DMA
    return pl.pallas_call(
        functools.partial(kernel, n, row_total),
        out_shape=jax.ShapeDtypeStruct(latents.shape, BF16),
        in_specs=[anywhere, anywhere, smem, smem, vmem, vmem, vmem] + [anywhere] * 7,
        out_specs=anywhere,
        scratch_shapes=[
            pltpu.VMEM(latents.shape, BF16),
            dma((frames_dev,)),
            pltpu.VMEM(condition.shape, BF16),
            pltpu.VMEM((9,) + square, BF16),
            pltpu.VMEM(square, BF16),
            pltpu.VMEM(square, BF16),
            pltpu.VMEM(square, BF16),
            pltpu.VMEM(square, BF16),
            pltpu.VMEM(square, BF16),
            pltpu.VMEM((9,) + square, BF16),
            pltpu.VMEM((frames, pix, channels), BF16),
            pltpu.VMEM((slots, n, pix, channels), BF16),
            [pltpu.VMEM((slots * n, chunk, channels), BF16) for _ in range(chunks)],
            pltpu.VMEM((frames, pix, channels), F32),
            pltpu.VMEM((pieces, frames, group, channels), BF16),
            pltpu.VMEM((frames_dev, n, pieces, group, channels), BF16),
            pltpu.VMEM((frames_dev, rows, per_row, pieces, group, channels), BF16),
            pltpu.VMEM((slots, cols, channels), BF16),
            pltpu.VMEM((slots, cols, channels), BF16),
            pltpu.VMEM((frames_dev, per_row, pieces, group, channels), BF16),
            pltpu.VMEM((frames_dev, per_row, pieces, group, channels), BF16),
            pltpu.VMEM((3, slots, rows, cols, channels), F32),
            pltpu.VMEM((3, frames_dev, rows, cols, channels), F32),
            dma((8,)),
            dma((1 + chunks + pieces,)),
            dma((n,)),
            dma((n,)),
            dma((chunks, n)),
            dma((chunks, n)),
            dma((pieces, n)),
            dma((pieces, n)),
            dma((2,)),
            dma((2,)),
            dma((2, pieces)),
            dma((2, pieces)),
        ],
        compiler_params=pltpu.CompilerParams(
            collective_id=0, has_side_effects=True, vmem_limit_bytes=60 * 1024 * 1024
        ),
    )(
        latents.reshape(frames_dev, n, pix, channels),
        condition,
        key_frames,
        propagate,
        encoding,
        attention_gain,
        conv_gain,
        encoder_conv,
        zero_conv,
        query_weight,
        key_weight,
        value_weight,
        output_weight,
        block_conv,
    )


def solution(mesh):
    placed = (
        P(("group", "frame"), "row", None, None),
        P(("group", "frame"), "row", None, None),
        P("group"),
        P("group"),
        P(),
        P(),
        P(),
        P(),
        P(),
        P(),
        P(),
        P(),
        P(),
    )
    return jax.shard_map(
        shards,
        mesh=mesh,
        in_specs=placed,
        out_specs=P(("group", "frame"), "row", None, None),
        check_vma=False,
    )
```

profile of v0, /device:TPU:0, one launch (start us, length us, event | category | flops | bytes accessed | tf_op | source)
XLA Modules:
  0.0 35.8 jit_solution(16446087648846159132)
XLA Ops:
  0.0 33.9 %shard_map.136 = bf16[6,2,64,320]{3,2,1,0:T(8,128)(2,1)} custom-call(bf16[6,4,32,320]{3,2,1,0:T(8,128)(2,1)} %bitcast.1, bf16[3,2,64,320]{3,2,1,0:T(8,128)(2,1)} %cond_hbm.1, s32[12]{0:T(128)} %key_frames.1, s32[24]{0:T(128)} %propagate.1, f32[24,320]{1,0:T(8,128)} %constant.2.clone.encoding, f32[320]{0:T(512)} %gain_a.1, f32[320]{0:T(512)} %gain_c.1, ...), custom_call_target="tpu_custom_call" | custom-call | tf_op jit(solution)/shard_map/pallas_call | solution.py:442
  33.9 1.9 %copy.16 = bf16[6,2,64,320]{3,2,1,0:T(8,128)(2,1)} copy(bf16[6,2,64,320]{3,2,1,0:T(8,128)(2,1)} %shard_map.136) | data formatting | bytes 983040
where the time goes:
time: 36.1 us; the launch traced here: 35.8 us
  Pallas kernels  33.9 us (94%)
  local copies, waits for them, and re-layouts  1.94 us (5%)
    pallas_call x1, Pallas kernels, shards(): pl.pallas_call(functools.partial(kernel, n, row_total), out_shape=jax.Sha...  33.9 us
    unnamed x1, local copies, waits for them, and re-layouts  1.94 us

commit v1 on v0

v1 whole, which is shorter than its diff:
```python
import functools
import math

import jax
import jax.numpy as jnp
import numpy as np
from jax import lax
from jax.experimental import pallas as pl
from jax.experimental.pallas import tpu as pltpu
from jax.sharding import PartitionSpec as P

HEADS = 8
MESH = pl.DeviceIdType.MESH
F32 = jnp.float32
BF16 = jnp.bfloat16


def positions(frame_total, channels):
    frame_pos = np.arange(frame_total, dtype=np.float64)[:, None]
    half_index = np.arange(channels // 2, dtype=np.float64)
    frequency = np.exp(half_index * (-2.0 * math.log(10000.0) / channels))
    angles = frame_pos * frequency
    stacked = np.stack([np.sin(angles), np.cos(angles)], axis=-1)
    return stacked.reshape(frame_total, channels).astype(np.float32)


def norm(values, gain):
    average = jnp.mean(values, axis=-1, keepdims=True)
    centered = values - average
    variance = jnp.mean(centered * centered, axis=-1, keepdims=True)
    return centered * lax.rsqrt(variance + 1e-05) * gain


def silu(values):
    half = 0.5 * values
    return half + half * jnp.tanh(half)


def dot(left, right):
    return jnp.dot(left, right, preferred_element_type=F32)


def dot_nt(left, right):
    return lax.dot_general(left, right, (((1,), (1,)), ((), ())), preferred_element_type=F32)


def flat(values):
    return values.astype(F32).reshape(-1, values.shape[-1]).astype(BF16)


def pack_rows(values):
    size = values.shape[1]
    whole = values.shape[2] // 128 * 128
    parts = [values[:, :, low : low + 128] for low in range(0, whole, 128)]
    tail = values[:, :, whole:]
    if size % 16 == 0:
        parts.append(jnp.concatenate([tail[:, : size // 2], tail[:, size // 2 :]], axis=2))
    else:
        parts.append(jnp.concatenate([tail, jnp.zeros_like(tail)], axis=2))
    return jnp.concatenate(parts, axis=1)


def packed_size(size, channels):
    return size * (channels // 128) + (size // 2 if size % 16 == 0 else size)


def unpack_rows(ref, index, size, channels, low, count):
    whole = channels // 128
    rest = channels - whole * 128
    def take(start, rows):
        if isinstance(index, tuple):
            return ref[index[0], :, start : start + rows].astype(F32)
        return ref[index, start : start + rows].astype(F32)

    parts = [take(i * size + low, count) for i in range(whole)]
    if size % 16:
        tail = take(whole * size + low, count)[..., :rest]
    else:
        half = size // 2
        start = low % half
        tile = take(whole * size + start, min(count, half))
        if count == size:
            tail = jnp.concatenate([tile[..., :rest], tile[..., rest:]], axis=-2)
        else:
            tail = tile[..., :rest] if low < half else tile[..., rest:]
    return jnp.concatenate(parts + [tail], axis=-1)


def pack_lead(values):
    count = values.shape[0]
    whole = values.shape[2] // 128 * 128
    parts = [values[:, :, low : low + 128] for low in range(0, whole, 128)]
    tail = values[:, :, whole:]
    parts.append(jnp.concatenate([tail[: count // 2], tail[count // 2 :]], axis=2))
    return jnp.concatenate(parts, axis=0)


def unpack_lead(values, count, channels):
    whole = channels // 128
    rest = channels - whole * 128
    parts = [values[i * count : (i + 1) * count] for i in range(whole)]
    tile = values[whole * count :]
    parts.append(jnp.concatenate([tile[..., :rest], tile[..., rest:]], axis=0))
    return jnp.concatenate(parts, axis=-1)


def pack_tails(tails, packed, main):
    wide = 3 * main
    for a in range(3):
        parts = [tails[3 * a + b] for b in range(3)]
        packed[a, :, wide:] = jnp.concatenate(parts, axis=1)


def conv_local(images, packed, put, add):
    rows = images.shape[1]
    put(slice(0, rows), dot(flat(images), packed[1]))
    if rows > 1:
        add(slice(1, rows), dot(flat(images[:, : rows - 1]), packed[0]))
        add(slice(0, rows - 1), dot(flat(images[:, 1:]), packed[2]))


def pair_tiles(weight, width):
    rows, channels = weight.shape
    tiles = []
    for low in range(0, channels, width):
        tiles.append(weight[:, low : low + width])
        tiles.append(jnp.zeros((rows, 128 - width), weight.dtype))
    return jnp.concatenate(tiles, axis=1)


def conv_row(total, main, tail):
    cols = total.shape[0]
    col = lax.broadcasted_iota(jnp.int32, (cols, 1), 0)
    pieces = []
    for start, size in ((0, main), (3 * main, tail)):
        left, middle, right = (total[:, start + b * size : start + (b + 1) * size] for b in range(3))
        left = jnp.where(col == 0, 0.0, pltpu.roll(left, 1, 0))
        right = jnp.where(col == cols - 1, 0.0, pltpu.roll(right, cols - 1, 0))
        pieces.append(left + middle + right)
    return jnp.concatenate(pieces, axis=1)


def kernel(
    n,
    row_total,
    lat,
    cond_hbm,
    key_hbm,
    prop_hbm,
    encoding_hbm,
    gain_a_hbm,
    gain_c_hbm,
    enc_hbm,
    zero_hbm,
    q_hbm,
    k_hbm,
    v_hbm,
    o_hbm,
    blk_hbm,
    out,
    key_frames,
    propagate,
    encoding,
    gain_a,
    gain_c,
    cond,
    enc_w,
    enc_t,
    zero_w,
    q_w,
    k_w,
    v_w,
    o_w,
    blk_w,
    blk_t,
    v_wt,
    q_wp,
    k_wp,
    q_both,
    k_held,
    v_held,
    scores,
    probs,
    mixed_t,
    lat_own,
    lat_out,
    lat_pix,
    res_out,
    res_pix,
    hidden,
    att_out,
    att_in,
    att,
    act,
    cond_out,
    cond_top,
    cond_bot,
    act_out,
    act_top,
    act_bot,
    sums_e,
    sums_b,
    w_sem,
    send,
    lat_recv,
    res_recv,
    att_recv,
    ch_recv,
    ah_recv,
):
    me = lax.axis_index("frame")
    row_me = lax.axis_index("row")
    frames_dev, _, pix, channels = lat.shape
    slots, rows, cols, _ = cond.shape
    chunks = res_recv.shape[0]
    chunk = pix // chunks
    frames = hidden.shape[0]
    pieces, group = att.shape[2:4]
    per_chunk = chunk // group
    per_row = n // rows
    head_dim = channels // HEADS
    main = enc_w.shape[2] // 3 // 128 * 128
    tail = channels - main
    has_up = row_me > 0
    has_down = row_me < row_total - 1

    barrier = pltpu.get_barrier_semaphore()
    for k in range(1, n):
        pl.semaphore_signal(
            barrier, inc=1, device_id={"frame": lax.rem(me + k, n)}, device_id_type=MESH
        )

    @pl.when(has_up)
    def _():
        pl.semaphore_signal(barrier, inc=1, device_id={"row": row_me - 1}, device_id_type=MESH)

    @pl.when(has_down)
    def _():
        pl.semaphore_signal(barrier, inc=1, device_id={"row": row_me + 1}, device_id_type=MESH)

    def start_taps(src, packed, sem):
        for a in range(3):
            for b in range(3):
                pltpu.make_async_copy(
                    src.at[3 * a + b, :, :main], packed.at[a, :, b * main : (b + 1) * main], sem
                ).start()

    def wait_taps(packed, sem):
        whole = packed.at[:, :, : 3 * main]
        pltpu.make_async_copy(whole, whole, sem).wait()

    pairs = [
        (cond_hbm, cond),
        (enc_hbm.at[:, :, main:], enc_t),
        (v_hbm, v_w),
        (zero_hbm, zero_w),
        (q_hbm, q_w),
        (k_hbm, k_w),
        (o_hbm, o_w),
        (encoding_hbm, encoding),
        (gain_a_hbm, gain_a),
        (gain_c_hbm, gain_c),
        (key_hbm, key_frames),
        (prop_hbm, propagate),
        (blk_hbm.at[:, :, main:], blk_t),
        (lat, lat_own),
    ]
    loads = [pltpu.make_async_copy(s, d, w_sem.at[2 + i]) for i, (s, d) in enumerate(pairs)]
    loads[0].start()
    loads[13].start()
    loads[1].start()
    start_taps(enc_hbm, enc_w, w_sem.at[0])

    @pl.when(jnp.logical_not(has_up))
    def _():
        cond_top[...] = jnp.zeros_like(cond_top)
        act_top[...] = jnp.zeros_like(act_top)

    @pl.when(jnp.logical_not(has_down))
    def _():
        cond_bot[...] = jnp.zeros_like(cond_bot)
        act_bot[...] = jnp.zeros_like(act_bot)

    loads[0].wait()
    cond_out[0] = pack_rows(cond[:, 0].astype(F32)).astype(BF16)
    cond_out[1] = pack_rows(cond[:, rows - 1].astype(F32)).astype(BF16)
    loads[13].wait()
    for p in range(n):
        lat_out[p] = pack_rows(lat_own[:, p].astype(F32)).astype(BF16)

    neighbours = has_up.astype(jnp.int32) + has_down.astype(jnp.int32)
    with jax.named_scope("w_barrier"):
        pl.semaphore_wait(barrier, n - 1 + neighbours)

    def remote(src, dst, send_sem, recv_sem, **where):
        return pltpu.make_async_remote_copy(
            src_ref=src,
            dst_ref=dst,
            send_sem=send_sem,
            recv_sem=recv_sem,
            device_id=where,
            device_id_type=MESH,
        )

    def up(src, dst, send_sem, recv_sem):
        return remote(src, dst, send_sem, recv_sem, row=row_me - 1)

    def down(src, dst, send_sem, recv_sem):
        return remote(src, dst, send_sem, recv_sem, row=row_me + 1)

    def drain(ref, sem):
        pltpu.make_async_copy(ref, ref, sem).wait()

    cond_up = up(cond_out.at[0], cond_bot, send.at[0], ch_recv.at[0])
    cond_down = down(cond_out.at[1], cond_top, send.at[1], ch_recv.at[1])
    pl.when(has_up)(cond_up.start)
    pl.when(has_down)(cond_down.start)

    peers = [lax.rem(me + k, n) for k in range(1, n)]
    for peer in peers:
        remote(
            lat_out.at[peer],
            lat_pix.at[pl.ds(me * frames_dev, frames_dev)],
            send.at[2],
            lat_recv.at[0],
            frame=peer,
        ).start()
    lat_pix[pl.ds(me * frames_dev, frames_dev)] = lat_out[me]
    for load in loads[2:13]:
        load.start()
    start_taps(blk_hbm, blk_w, w_sem.at[1])

    with jax.named_scope("w_load01"):
        loads[1].wait()
    with jax.named_scope("pack_enc"):
        pack_tails(enc_t, enc_w, main)
        wait_taps(enc_w, w_sem.at[0])

    def edge_rows(ref, index, size):
        values = unpack_rows(ref, index, size, channels, 0, size)
        return values.reshape(-1, channels).astype(BF16)

    def put_e(r, value):
        sums_e[:, r] = value.reshape(slots, -1, cols, value.shape[-1])

    def add_e(r, value):
        sums_e[:, r] += value.reshape(slots, -1, cols, value.shape[-1])

    with jax.named_scope("encconv_local"):
        conv_local(cond[...], enc_w, put_e, add_e)
    with jax.named_scope("prep"):
        loads[2].wait()
        v_wt[...] = jnp.transpose(v_w[...].astype(F32)).astype(BF16)
        for load in loads[4:6]:
            load.wait()
        q_wp[...] = pair_tiles(q_w[...], 2 * head_dim)
        k_wp[...] = pair_tiles(k_w[...], 2 * head_dim)
        loads[12].wait()
        pack_tails(blk_t, blk_w, main)
    with jax.named_scope("w_condhalo"):
        pl.when(has_up)(cond_down.wait_recv)
        pl.when(has_down)(cond_up.wait_recv)
    with jax.named_scope("encconv_edge"):
        add_e(slice(0, 1), dot(edge_rows(cond_top, slice(None), cols), enc_w[0]))
        add_e(slice(rows - 1, rows), dot(edge_rows(cond_bot, slice(None), cols), enc_w[2]))
    with jax.named_scope("enc_silu_zero"):
        loads[3].wait()
        encoded = jnp.concatenate(
            [silu(conv_row(sums_e[s, r], main, tail)) for s in range(slots) for r in range(rows)],
            axis=0,
        ).astype(BF16)
        keyres = dot(encoded, zero_w[...]).reshape(slots, n, pix, channels)
        for p in range(n):
            for c in range(chunks):
                part = pack_rows(keyres[:, p, c * chunk : (c + 1) * chunk])
                res_out[p, c] = part.astype(BF16)
    for c in range(chunks):
        for peer in peers:
            remote(
                res_out.at[peer, c],
                res_pix[c].at[pl.ds(me * slots, slots)],
                send.at[3],
                res_recv.at[c],
                frame=peer,
            ).start()
    for c in range(chunks):
        res_pix[c][pl.ds(me * slots, slots)] = res_out[me, c]

    with jax.named_scope("w_loads"):
        for load in loads[6:12]:
            load.wait()
    with jax.named_scope("w_lat"):
        drain(lat_pix.at[: (n - 1) * frames_dev], lat_recv.at[0])

    small = frames <= 24
    block = frames * group
    factor = math.log2(math.e) / math.sqrt(head_dim)
    encode = encoding[...][:, None, :]
    lane = lax.broadcasted_iota(jnp.int32, (1, 128), 1)
    pairs_total = HEADS // 2

    def soft(values):
        width = values.shape[-1]
        values = values.reshape(frames, group, width)
        top = jnp.max(values, axis=0, keepdims=True)
        powers = jnp.exp2(values - top)
        total = jnp.sum(powers, axis=0, keepdims=True)
        pixel = lax.broadcasted_iota(jnp.int32, (1, group, width), 1)
        query = lax.broadcasted_iota(jnp.int32, (1, group, width), 2)
        weight = jnp.where(lax.rem(query, group) == pixel, 1.0 / total, 0.0)
        return (powers * weight).reshape(block, width).astype(BF16)

    def hide(c):
        span = slice(c * chunk, (c + 1) * chunk)
        drain(res_pix[c].at[: (n - 1) * slots], res_recv.at[c])

        def one(f, carry):
            slot = propagate[f]
            gap = jnp.abs(f - key_frames[slot]).astype(F32)
            reach = jnp.exp(jnp.full((1, channels), -gap / (2 * frames_dev), F32))
            residual = unpack_rows(res_pix[c], slot, chunk, channels, 0, chunk)
            value = unpack_rows(lat_pix, f, pix, channels, c * chunk, chunk) + reach * residual
            hidden[f, span] = value.astype(BF16).astype(F32)
            return carry

        lax.fori_loop(0, frames, one, 0, unroll=small)

    def project(s):
        if s % per_chunk == 0:
            hide(s // per_chunk)
        base = hidden[:, s * group : (s + 1) * group]
        normed = (norm(base, gain_a[...]) + encode).reshape(block, channels).astype(BF16)
        query = dot(normed, q_wp[...]) * factor
        for j in range(pairs_total):
            tile = query[:, 128 * j : 128 * (j + 1)]
            q_both[s % 2, j, :block] = jnp.where(lane < head_dim, tile, 0.0).astype(BF16)
            q_both[s % 2, j, block:] = jnp.where(lane < head_dim, 0.0, tile).astype(BF16)
        k_held[s % 2] = dot(normed, k_wp[...]).astype(BF16)
        v_held[s % 2] = dot_nt(v_wt[...], normed).astype(BF16)

    def score(s, j):
        keys = k_held[s % 2, :, 128 * j : 128 * (j + 1)]
        scores[j % 2] = dot_nt(keys, q_both[s % 2, j])

    def soften(s, j):
        probs[j % 2] = soft(scores[j % 2])

    def mix(s, j):
        low, high = 2 * j * head_dim, 2 * (j + 1) * head_dim
        pair = dot(v_held[s % 2, low:high], probs[j % 2])
        mixed_t[low : low + head_dim] = pair[:head_dim, :block]
        mixed_t[low + head_dim : high] = pair[head_dim:, block:]

    def finish(s):
        mixed = jnp.transpose(mixed_t[...]).astype(BF16)
        projected = dot(mixed, o_w[...]).reshape(frames, group, channels)
        base = hidden[:, s * group : (s + 1) * group]
        total = base + projected
        for p in range(n):
            part = pack_lead(total[p * frames_dev : (p + 1) * frames_dev])
            att_out[s, p] = part.astype(BF16)
        for peer in peers:
            remote(
                att_out.at[s, peer],
                att_in.at[me, s],
                send.at[4],
                att_recv.at[s],
                frame=peer,
            ).start()
        att_in[me, s] = att_out[s, me]

    with jax.named_scope("attention"):
        if small:
            steps = [(s, j) for s in range(pieces) for j in range(pairs_total)]
            project(0)
            score(*steps[0])
            for k, (s, j) in enumerate(steps):
                if k + 1 < len(steps):
                    score(*steps[k + 1])
                soften(s, j)
                if k > 0:
                    mix(*steps[k - 1])
                    if steps[k - 1][1] == pairs_total - 1:
                        finish(steps[k - 1][0])
                if j == 1 and s + 1 < pieces:
                    project(s + 1)
            mix(*steps[-1])
            finish(pieces - 1)
        else:
            for s in range(pieces):
                project(s)

                def step(j, carry):
                    keys = k_held[s % 2, :, pl.ds(pl.multiple_of(128 * j, 128), 128)]
                    for i in range(2):
                        part = q_both[s % 2, j, i * block : (i + 1) * block]
                        row = pl.ds(pl.multiple_of((2 * j + i) * head_dim, 8), head_dim)
                        value = dot(v_held[s % 2], soft(dot_nt(keys, part)))
                        scores[0, :channels, :block] = value
                        mixed_t[row] = scores[0, row, :block]
                    return carry

                lax.fori_loop(0, pairs_total, step, 0)
                finish(s)

    def add_b(r, span, ref, taps):
        parts = [edge_rows(ref, (s,), per_row * group) for s in range(span.start, span.stop)]
        value = dot(jnp.concatenate(parts, axis=0), taps)
        value = value.reshape(len(parts), frames_dev, per_row, group, value.shape[-1])
        for i, s in enumerate(range(span.start, span.stop)):
            sums_b[:, r, :, s] += value[i]

    def put_all(r, value):
        sums_b[:, r] = value.reshape(frames_dev, -1, per_row, pieces, group, value.shape[-1])

    def add_all(r, value):
        sums_b[:, r] += value.reshape(frames_dev, -1, per_row, pieces, group, value.shape[-1])

    act_ups, act_downs = [], []
    for s in range(pieces):
        with jax.named_scope(f"w_att{s}"):
            drain(att_in.at[: n - 1, s], att_recv.at[s])
        with jax.named_scope(f"act{s}"):
            taken = [unpack_lead(att_in[p, s].astype(F32), frames_dev, channels) for p in range(n)]
            value = jnp.stack(taken, axis=1)
            att[:, :, s] = value.astype(BF16)
            value = silu(norm(value, gain_c[...])).reshape(frames_dev, rows, -1, channels)
            act_out[0, s] = pack_rows(value[:, 0]).astype(BF16)
            act_out[1, s] = pack_rows(value[:, rows - 1]).astype(BF16)
            value = value.reshape(frames_dev, rows, per_row, group, channels)
            act[:, :, :, s] = value.astype(BF16)
        act_up = up(act_out.at[0, s], act_bot.at[s], send.at[5], ah_recv.at[0, s])
        act_down = down(
            act_out.at[1, s], act_top.at[s], send.at[6], ah_recv.at[1, s]
        )
        pl.when(has_up)(act_up.start)
        pl.when(has_down)(act_down.start)
        act_ups.append(act_up)
        act_downs.append(act_down)
    wait_taps(blk_w, w_sem.at[1])
    with jax.named_scope("blkconv_local"):
        conv_local(act[...].reshape(frames_dev, rows, -1, group, channels), blk_w, put_all, add_all)
    last = max(pieces - 1, 0)
    for span in [slice(0, last), slice(last, pieces)] if last else [slice(0, pieces)]:
        with jax.named_scope(f"w_acthalo{span.start}"):
            for s in range(span.start, span.stop):
                pl.when(has_up)(act_downs[s].wait_recv)
                pl.when(has_down)(act_ups[s].wait_recv)
        with jax.named_scope(f"blkconv_edge{span.start}"):
            add_b(0, span, act_top, blk_w[0])
            add_b(rows - 1, span, act_bot, blk_w[2])
    with jax.named_scope("final"):
        for f in range(frames_dev):
            for r in range(rows):
                convolved = conv_row(sums_b[f, r].reshape(cols, -1), main, tail)
                held = att[f, r * per_row : (r + 1) * per_row].astype(F32).reshape(cols, channels)
                out[f, r] = (held + convolved).astype(BF16)
    with jax.named_scope("w_end"):
        pl.when(has_up)(cond_up.wait_send)
        pl.when(has_down)(cond_down.wait_send)
        drain(lat_pix.at[: (n - 1) * frames_dev], send.at[2])
        drain(res_out.at[: n - 1], send.at[3])
        drain(att_out.at[:, : n - 1], send.at[4])
        pl.when(has_up)(lambda: drain(act_out.at[0], send.at[5]))
        pl.when(has_down)(lambda: drain(act_out.at[1], send.at[6]))


def shards(
    latents,
    condition,
    key_frames,
    propagate,
    encoder_conv,
    zero_conv,
    attention_gain,
    query_weight,
    key_weight,
    value_weight,
    output_weight,
    conv_gain,
    block_conv,
):
    frames_dev, rows, cols, channels = latents.shape
    slots = condition.shape[0]
    n = lax.axis_size("frame")
    row_total = lax.axis_size("row")
    pix = rows * cols // n
    frames = frames_dev * n
    chunk = 16 if pix % 16 == 0 else 8
    chunks = pix // chunk
    group = 8
    pieces = pix // group
    block = frames * group
    per_row = n // rows
    main = channels // 256 * 256
    tail = channels - main
    wide = 3 * (main + tail)
    lat_size = packed_size(pix, channels)
    res_size = packed_size(chunk, channels)
    cond_size = packed_size(cols, channels)
    act_size = packed_size(per_row * group, channels)
    att_size = frames_dev * (channels // 128) + frames_dev // 2
    encoding = jnp.asarray(positions(frames, channels))
    square = (channels, channels)
    dma = pltpu.SemaphoreType.DMA
    values = [
        latents.reshape(frames_dev, n, pix, channels),
        condition,
        key_frames,
        propagate,
        encoding,
        attention_gain,
        conv_gain,
        encoder_conv,
        zero_conv,
        query_weight,
        key_weight,
        value_weight,
        output_weight,
        block_conv,
    ]
    values = [pltpu.with_memory_space_constraint(v, pltpu.MemorySpace.HBM) for v in values]
    return pl.pallas_call(
        functools.partial(kernel, n, row_total),
        out_shape=pltpu.VMEM(latents.shape, BF16),
        in_specs=[pl.BlockSpec(memory_space=pl.ANY)] * len(values),
        out_specs=pl.BlockSpec(memory_space=pltpu.VMEM),
        scratch_shapes=[
            pltpu.SMEM(key_frames.shape, jnp.int32),
            pltpu.SMEM(propagate.shape, jnp.int32),
            pltpu.VMEM((frames, channels), F32),
            pltpu.VMEM((channels,), F32),
            pltpu.VMEM((channels,), F32),
            pltpu.VMEM(condition.shape, BF16),
            pltpu.VMEM((3, channels, wide), BF16),
            pltpu.VMEM((9, channels, tail), BF16),
            pltpu.VMEM(square, BF16),
            pltpu.VMEM(square, BF16),
            pltpu.VMEM(square, BF16),
            pltpu.VMEM(square, BF16),
            pltpu.VMEM(square, BF16),
            pltpu.VMEM((3, channels, wide), BF16),
            pltpu.VMEM((9, channels, tail), BF16),
            pltpu.VMEM(square, BF16),
            pltpu.VMEM((channels, 64 * HEADS), BF16),
            pltpu.VMEM((channels, 64 * HEADS), BF16),
            pltpu.VMEM((2, HEADS // 2, 2 * block, 128), BF16),
            pltpu.VMEM((2, block, 64 * HEADS), BF16),
            pltpu.VMEM((2, channels, block), BF16),
            pltpu.VMEM((2, block, 2 * block), F32),
            pltpu.VMEM((2, block, 2 * block), BF16),
            pltpu.VMEM((channels, block), F32),
            pltpu.VMEM((frames_dev, n, pix, channels), BF16),
            pltpu.VMEM((n, frames_dev, lat_size, 128), BF16),
            pltpu.VMEM((frames, lat_size, 128), BF16),
            pltpu.VMEM((n, chunks, slots, res_size, 128), BF16),
            [pltpu.VMEM((slots * n, res_size, 128), BF16) for _ in range(chunks)],
            pltpu.VMEM((frames, pix, channels), F32),
            pltpu.VMEM((pieces, n, att_size, group, 128), BF16),
            pltpu.VMEM((n, pieces, att_size, group, 128), BF16),
            pltpu.VMEM((frames_dev, n, pieces, group, channels), BF16),
            pltpu.VMEM((frames_dev, rows, per_row, pieces, group, channels), BF16),
            pltpu.VMEM((2, slots, cond_size, 128), BF16),
            pltpu.VMEM((slots, cond_size, 128), BF16),
            pltpu.VMEM((slots, cond_size, 128), BF16),
            pltpu.VMEM((2, pieces, frames_dev, act_size, 128), BF16),
            pltpu.VMEM((pieces, frames_dev, act_size, 128), BF16),
            pltpu.VMEM((pieces, frames_dev, act_size, 128), BF16),
            pltpu.VMEM((slots, rows, cols, wide), F32),
            pltpu.VMEM((frames_dev, rows, per_row, pieces, group, wide), F32),
            dma((16,)),
            dma((7,)),
            dma((1,)),
            dma((chunks,)),
            dma((pieces,)),
            dma((2,)),
            dma((2, pieces)),
        ],
        compiler_params=pltpu.CompilerParams(
            collective_id=0, has_side_effects=True, vmem_limit_bytes=48 * 1024 * 1024
        ),
    )(*values)


def solution(mesh):
    placed = (
        P(("group", "frame"), "row", None, None),
        P(("group", "frame"), "row", None, None),
        P("group"),
        P("group"),
        P(),
        P(),
        P(),
        P(),
        P(),
        P(),
        P(),
        P(),
        P(),
    )
    return jax.shard_map(
        shards,
        mesh=mesh,
        in_specs=placed,
        out_specs=P(("group", "frame"), "row", None, None),
        check_vma=False,
    )
```

time: 36.1 us -> 28.4 us (0.79)
  Pallas kernels: 33.9 us -> 27.4 us
  local copies, waits for them, and re-layouts: 1.94 us -> 0.82 us
    pallas_call x1, Pallas kernels: 33.9 us -> 27.4 us  [shards(): pl.pallas_call(functools.partial(kernel, n, row_total), out_shape=pltpu.V...]
    unnamed x1, local copies, waits for them, and re-layouts: 1.94 us -> 0.82 us
where the time goes in v1:
time: 28.4 us; the launch traced here: 28.2 us
  Pallas kernels  27.4 us (96%)
  local copies, waits for them, and re-layouts  0.82 us (3%)
    pallas_call x1, Pallas kernels, shards(): pl.pallas_call(functools.partial(kernel, n, row_total), out_shape=pltpu.V...  27.4 us
    unnamed x1, local copies, waits for them, and re-layouts  0.82 us

profile of v1, /device:TPU:0, one launch (start us, length us, event | category | flops | bytes accessed | tf_op | source)
XLA Modules:
  0.0 28.2 jit_solution(61279105393209073)
XLA Ops:
  0.0 27.4 %shard_map.136 = bf16[6,2,64,320]{3,2,1,0:T(8,128)(2,1)S(1)} custom-call(bf16[6,4,32,320]{3,2,1,0:T(8,128)(2,1)} %bitcast.1, bf16[3,2,64,320]{3,2,1,0:T(8,128)(2,1)} %cond_hbm.1, s32[12]{0:T(128)} %key_hbm.1, s32[24]{0:T(128)} %prop_hbm.1, f32[24,320]{1,0:T(8,128)} %constant.2.clone.encoding_hbm, f32[320]{0:T(512)} %gain_a_hbm.1, f32[320]{0:T(512)} %gain_c_hbm.1, ...), custom_call_target="tpu_custom_call" | custom-call | tf_op jit(solution)/shard_map/pallas_call | solution.py:623
  27.4 0.8 %copy.16 = bf16[6,2,64,320]{3,2,1,0:T(8,128)(2,1)} copy(bf16[6,2,64,320]{3,2,1,0:T(8,128)(2,1)S(1)} %shard_map.136) | data formatting | bytes 983040

commit v2 on v1

--- a/solution.py
+++ b/solution.py
@@ -157,7 +157,8 @@
     v_hbm,
     o_hbm,
     blk_hbm,
-    out,
+    sums_b,
+    att,
     key_frames,
     propagate,
     encoding,
@@ -166,16 +167,13 @@
     cond,
     enc_w,
     enc_t,
-    zero_w,
-    q_w,
-    k_w,
-    v_w,
-    o_w,
+    squares,
     blk_w,
     blk_t,
     v_wt,
     q_wp,
     k_wp,
+    normed,
     q_both,
     k_held,
     v_held,
@@ -190,7 +188,6 @@
     hidden,
     att_out,
     att_in,
-    att,
     act,
     cond_out,
     cond_top,
@@ -199,7 +196,6 @@
     act_top,
     act_bot,
     sums_e,
-    sums_b,
     w_sem,
     send,
     lat_recv,
@@ -251,25 +247,19 @@
 
     pairs = [
         (cond_hbm, cond),
+        (lat, lat_own),
         (enc_hbm.at[:, :, main:], enc_t),
-        (v_hbm, v_w),
-        (zero_hbm, zero_w),
-        (q_hbm, q_w),
-        (k_hbm, k_w),
-        (o_hbm, o_w),
+        (blk_hbm.at[:, :, main:], blk_t),
         (encoding_hbm, encoding),
         (gain_a_hbm, gain_a),
         (gain_c_hbm, gain_c),
         (key_hbm, key_frames),
         (prop_hbm, propagate),
-        (blk_hbm.at[:, :, main:], blk_t),
-        (lat, lat_own),
     ]
-    loads = [pltpu.make_async_copy(s, d, w_sem.at[2 + i]) for i, (s, d) in enumerate(pairs)]
+    loads = [pltpu.make_async_copy(s, d, w_sem.at[3 + i]) for i, (s, d) in enumerate(pairs)]
     loads[0].start()
-    loads[13].start()
     loads[1].start()
-    start_taps(enc_hbm, enc_w, w_sem.at[0])
+    loads[2].start()
 
     @pl.when(jnp.logical_not(has_up))
     def _():
@@ -281,13 +271,10 @@
         cond_bot[...] = jnp.zeros_like(cond_bot)
         act_bot[...] = jnp.zeros_like(act_bot)
 
+    start_taps(enc_hbm, enc_w, w_sem.at[0])
     loads[0].wait()
     cond_out[0] = pack_rows(cond[:, 0].astype(F32)).astype(BF16)
     cond_out[1] = pack_rows(cond[:, rows - 1].astype(F32)).astype(BF16)
-    loads[13].wait()
-    for p in range(n):
-        lat_out[p] = pack_rows(lat_own[:, p].astype(F32)).astype(BF16)
-
     neighbours = has_up.astype(jnp.int32) + has_down.astype(jnp.int32)
     with jax.named_scope("w_barrier"):
         pl.semaphore_wait(barrier, n - 1 + neighbours)
@@ -316,6 +303,9 @@
     pl.when(has_up)(cond_up.start)
     pl.when(has_down)(cond_down.start)
 
+    loads[1].wait()
+    for p in range(n):
+        lat_out[p] = pack_rows(lat_own[:, p].astype(F32)).astype(BF16)
     peers = [lax.rem(me + k, n) for k in range(1, n)]
     for peer in peers:
         remote(
@@ -326,12 +316,14 @@
             frame=peer,
         ).start()
     lat_pix[pl.ds(me * frames_dev, frames_dev)] = lat_out[me]
-    for load in loads[2:13]:
+    for i, source in enumerate((v_hbm, zero_hbm, q_hbm, k_hbm, o_hbm)):
+        pltpu.make_async_copy(source, squares.at[i], w_sem.at[2]).start()
+    for load in loads[3:]:
         load.start()
     start_taps(blk_hbm, blk_w, w_sem.at[1])
 
     with jax.named_scope("w_load01"):
-        loads[1].wait()
+        loads[2].wait()
     with jax.named_scope("pack_enc"):
         pack_tails(enc_t, enc_w, main)
         wait_taps(enc_w, w_sem.at[0])
@@ -349,13 +341,11 @@
     with jax.named_scope("encconv_local"):
         conv_local(cond[...], enc_w, put_e, add_e)
     with jax.named_scope("prep"):
-        loads[2].wait()
-        v_wt[...] = jnp.transpose(v_w[...].astype(F32)).astype(BF16)
-        for load in loads[4:6]:
-            load.wait()
-        q_wp[...] = pair_tiles(q_w[...], 2 * head_dim)
-        k_wp[...] = pair_tiles(k_w[...], 2 * head_dim)
-        loads[12].wait()
+        drain(squares, w_sem.at[2])
+        v_wt[...] = jnp.transpose(squares[0].astype(F32)).astype(BF16)
+        q_wp[...] = pair_tiles(squares[2], 2 * head_dim)
+        k_wp[...] = pair_tiles(squares[3], 2 * head_dim)
+        loads[3].wait()
         pack_tails(blk_t, blk_w, main)
     with jax.named_scope("w_condhalo"):
         pl.when(has_up)(cond_down.wait_recv)
@@ -364,12 +354,11 @@
         add_e(slice(0, 1), dot(edge_rows(cond_top, slice(None), cols), enc_w[0]))
         add_e(slice(rows - 1, rows), dot(edge_rows(cond_bot, slice(None), cols), enc_w[2]))
     with jax.named_scope("enc_silu_zero"):
-        loads[3].wait()
         encoded = jnp.concatenate(
             [silu(conv_row(sums_e[s, r], main, tail)) for s in range(slots) for r in range(rows)],
             axis=0,
         ).astype(BF16)
-        keyres = dot(encoded, zero_w[...]).reshape(slots, n, pix, channels)
+        keyres = dot(encoded, squares[1]).reshape(slots, n, pix, channels)
         for p in range(n):
             for c in range(chunks):
                 part = pack_rows(keyres[:, p, c * chunk : (c + 1) * chunk])
@@ -387,7 +376,7 @@
         res_pix[c][pl.ds(me * slots, slots)] = res_out[me, c]
 
     with jax.named_scope("w_loads"):
-        for load in loads[6:12]:
+        for load in loads[4:]:
             load.wait()
     with jax.named_scope("w_lat"):
         drain(lat_pix.at[: (n - 1) * frames_dev], lat_recv.at[0])
@@ -420,30 +409,47 @@
             reach = jnp.exp(jnp.full((1, channels), -gap / (2 * frames_dev), F32))
             residual = unpack_rows(res_pix[c], slot, chunk, channels, 0, chunk)
             value = unpack_rows(lat_pix, f, pix, channels, c * chunk, chunk) + reach * residual
-            hidden[f, span] = value.astype(BF16).astype(F32)
+            hidden[f, span] = value
             return carry
 
         lax.fori_loop(0, frames, one, 0, unroll=small)
 
+    mask = jnp.where(lane < head_dim, 1.0, 0.0).astype(BF16)
+    other = jnp.where(lane < head_dim, 0.0, 1.0).astype(BF16)
+
+    def prepare(s):
+        base = hidden[:, s * group : (s + 1) * group]
+        value = norm(base, gain_a[...]) + encode
+        normed[s % 2] = value.reshape(block, channels).astype(BF16)
+
+    def project_q(s, t):
+        query = dot(normed[s % 2], q_wp[:, 256 * t : 256 * (t + 1)]) * factor
+        query = query.astype(BF16)
+        for i in range(2):
+            tile = query[:, 128 * i : 128 * (i + 1)]
+            q_both[s % 2, 2 * t + i, :block] = tile * mask
+            q_both[s % 2, 2 * t + i, block:] = tile * other
+
+    def project_k(s, t):
+        keys = dot(normed[s % 2], k_wp[:, 256 * t : 256 * (t + 1)])
+        k_held[s % 2, :, 256 * t : 256 * (t + 1)] = keys.astype(BF16)
+
+    def project_v(s):
+        v_held[s % 2] = dot_nt(v_wt[...], normed[s % 2]).astype(BF16)
+
     def project(s):
-        if s % per_chunk == 0:
-            hide(s // per_chunk)
-        base = hidden[:, s * group : (s + 1) * group]
-        normed = (norm(base, gain_a[...]) + encode).reshape(block, channels).astype(BF16)
-        query = dot(normed, q_wp[...]) * factor
-        for j in range(pairs_total):
-            tile = query[:, 128 * j : 128 * (j + 1)]
-            q_both[s % 2, j, :block] = jnp.where(lane < head_dim, tile, 0.0).astype(BF16)
-            q_both[s % 2, j, block:] = jnp.where(lane < head_dim, 0.0, tile).astype(BF16)
-        k_held[s % 2] = dot(normed, k_wp[...]).astype(BF16)
-        v_held[s % 2] = dot_nt(v_wt[...], normed).astype(BF16)
+        prepare(s)
+        for t in range(pairs_total // 2):
+            project_q(s, t)
+            project_k(s, t)
+        project_v(s)
 
     def score(s, j):
         keys = k_held[s % 2, :, 128 * j : 128 * (j + 1)]
         scores[j % 2] = dot_nt(keys, q_both[s % 2, j])
 
-    def soften(s, j):
-        probs[j % 2] = soft(scores[j % 2])
+    def soften(s, j, low, high):
+        probs[j % 2, :, low:high] = soft(scores[j % 2, :, low:high])
 
     def mix(s, j):
         low, high = 2 * j * head_dim, 2 * (j + 1) * head_dim
@@ -453,7 +459,7 @@
 
     def finish(s):
         mixed = jnp.transpose(mixed_t[...]).astype(BF16)
-        projected = dot(mixed, o_w[...]).reshape(frames, group, channels)
+        projected = dot(mixed, squares[4]).reshape(frames, group, channels)
         base = hidden[:, s * group : (s + 1) * group]
         total = base + projected
         for p in range(n):
@@ -469,55 +475,7 @@
             ).start()
         att_in[me, s] = att_out[s, me]
 
-    with jax.named_scope("attention"):
-        if small:
-            steps = [(s, j) for s in range(pieces) for j in range(pairs_total)]
-            project(0)
-            score(*steps[0])
-            for k, (s, j) in enumerate(steps):
-                if k + 1 < len(steps):
-                    score(*steps[k + 1])
-                soften(s, j)
-                if k > 0:
-                    mix(*steps[k - 1])
-                    if steps[k - 1][1] == pairs_total - 1:
-                        finish(steps[k - 1][0])
-                if j == 1 and s + 1 < pieces:
-                    project(s + 1)
-            mix(*steps[-1])
-            finish(pieces - 1)
-        else:
-            for s in range(pieces):
-                project(s)
-
-                def step(j, carry):
-                    keys = k_held[s % 2, :, pl.ds(pl.multiple_of(128 * j, 128), 128)]
-                    for i in range(2):
-                        part = q_both[s % 2, j, i * block : (i + 1) * block]
-                        row = pl.ds(pl.multiple_of((2 * j + i) * head_dim, 8), head_dim)
-                        value = dot(v_held[s % 2], soft(dot_nt(keys, part)))
-                        scores[0, :channels, :block] = value
-                        mixed_t[row] = scores[0, row, :block]
-                    return carry
-
-                lax.fori_loop(0, pairs_total, step, 0)
-                finish(s)
-
-    def add_b(r, span, ref, taps):
-        parts = [edge_rows(ref, (s,), per_row * group) for s in range(span.start, span.stop)]
-        value = dot(jnp.concatenate(parts, axis=0), taps)
-        value = value.reshape(len(parts), frames_dev, per_row, group, value.shape[-1])
-        for i, s in enumerate(range(span.start, span.stop)):
-            sums_b[:, r, :, s] += value[i]
-
-    def put_all(r, value):
-        sums_b[:, r] = value.reshape(frames_dev, -1, per_row, pieces, group, value.shape[-1])
-
-    def add_all(r, value):
-        sums_b[:, r] += value.reshape(frames_dev, -1, per_row, pieces, group, value.shape[-1])
-
-    act_ups, act_downs = [], []
-    for s in range(pieces):
+    def activate(s):
         with jax.named_scope(f"w_att{s}"):
             drain(att_in.at[: n - 1, s], att_recv.at[s])
         with jax.named_scope(f"act{s}"):
@@ -529,32 +487,99 @@
             act_out[1, s] = pack_rows(value[:, rows - 1]).astype(BF16)
             value = value.reshape(frames_dev, rows, per_row, group, channels)
             act[:, :, :, s] = value.astype(BF16)
-        act_up = up(act_out.at[0, s], act_bot.at[s], send.at[5], ah_recv.at[0, s])
-        act_down = down(
-            act_out.at[1, s], act_top.at[s], send.at[6], ah_recv.at[1, s]
-        )
+        which = 1 if s == pieces - 1 else 0
+        act_up = up(act_out.at[0, s], act_bot.at[s], send.at[5], ah_recv.at[0, which])
+        act_down = down(act_out.at[1, s], act_top.at[s], send.at[6], ah_recv.at[1, which])
         pl.when(has_up)(act_up.start)
         pl.when(has_down)(act_down.start)
-        act_ups.append(act_up)
-        act_downs.append(act_down)
+
+    def attend_all():
+        turns = [(s, j) for s in range(pieces) for j in range(pairs_total)]
+        tiles = [(low, min(low + 128, 2 * block)) for low in range(0, 2 * block, 128)]
+        hide(0)
+        project(0)
+        score(0, 0)
+        for k, (s, j) in enumerate(turns):
+            work = []
+            if k > 0:
+                work.append(functools.partial(mix, *turns[k - 1]))
+            if k + 1 < len(turns) and j + 1 < pairs_total:
+                work.append(functools.partial(score, s, j + 1))
+            if j == 0 and s > 0:
+                work.append(functools.partial(finish, s - 1))
+            if s + 1 < pieces:
+                if j == 1:
+                    if (s + 1) % per_chunk == 0:
+                        hide((s + 1) // per_chunk)
+                    work.append(functools.partial(prepare, s + 1))
+                    work.append(functools.partial(project_q, s + 1, 0))
+                if j == 2:
+                    work.append(functools.partial(project_q, s + 1, 1))
+                    work.append(functools.partial(project_k, s + 1, 0))
+                if j == 3:
+                    work.append(functools.partial(project_k, s + 1, 1))
+                    work.append(functools.partial(project_v, s + 1))
+                    work.append(functools.partial(score, s + 1, 0))
+            for i in range(max(len(tiles), len(work))):
+                if i < len(tiles):
+                    soften(s, j, *tiles[i])
+                if i < len(work):
+                    work[i]()
+            if (pieces - s, j) == (1, 3) and pieces > 1:
+                activate(0)
+        mix(*turns[-1])
+        finish(pieces - 1)
+
+    with jax.named_scope("attention"):
+        if small:
+            attend_all()
+        else:
+            for s in range(pieces):
+                if s % per_chunk == 0:
+                    hide(s // per_chunk)
+                project(s)
+
+                def step(j, carry):
+                    keys = k_held[s % 2, :, pl.ds(pl.multiple_of(128 * j, 128), 128)]
+                    for i in range(2):
+                        part = q_both[s % 2, j, i * block : (i + 1) * block]
+                        row = pl.ds(pl.multiple_of((2 * j + i) * head_dim, 8), head_dim)
+                        value = dot(v_held[s % 2], soft(dot_nt(keys, part)))
+                        scores[0, :channels, :block] = value
+                        mixed_t[row] = scores[0, row, :block]
+                    return carry
+
+                lax.fori_loop(0, pairs_total, step, 0)
+                finish(s)
+
+    def add_b(r, span, ref, taps):
+        parts = [edge_rows(ref, (s,), per_row * group) for s in range(span.start, span.stop)]
+        value = dot(jnp.concatenate(parts, axis=0), taps)
+        value = value.reshape(len(parts), frames_dev, per_row, group, value.shape[-1])
+        for i, s in enumerate(range(span.start, span.stop)):
+            sums_b[:, r, :, s] += value[i]
+
+    def put_all(r, value):
+        sums_b[:, r] = value.reshape(frames_dev, -1, per_row, pieces, group, value.shape[-1])
+
+    def add_all(r, value):
+        sums_b[:, r] += value.reshape(frames_dev, -1, per_row, pieces, group, value.shape[-1])
+
+    early = 1 if small and pieces > 1 else 0
+    for s in range(early, pieces):
+        activate(s)
     wait_taps(blk_w, w_sem.at[1])
     with jax.named_scope("blkconv_local"):
         conv_local(act[...].reshape(frames_dev, rows, -1, group, channels), blk_w, put_all, add_all)
     last = max(pieces - 1, 0)
     for span in [slice(0, last), slice(last, pieces)] if last else [slice(0, pieces)]:
         with jax.named_scope(f"w_acthalo{span.start}"):
-            for s in range(span.start, span.stop):
-                pl.when(has_up)(act_downs[s].wait_recv)
-                pl.when(has_down)(act_ups[s].wait_recv)
+            which = 1 if span.stop == pieces else 0
+            pl.when(has_up)(lambda: drain(act_top.at[span], ah_recv.at[1, which]))
+            pl.when(has_down)(lambda: drain(act_bot.at[span], ah_recv.at[0, which]))
         with jax.named_scope(f"blkconv_edge{span.start}"):
             add_b(0, span, act_top, blk_w[0])
             add_b(rows - 1, span, act_bot, blk_w[2])
-    with jax.named_scope("final"):
-        for f in range(frames_dev):
-            for r in range(rows):
-                convolved = conv_row(sums_b[f, r].reshape(cols, -1), main, tail)
-                held = att[f, r * per_row : (r + 1) * per_row].astype(F32).reshape(cols, channels)
-                out[f, r] = (held + convolved).astype(BF16)
     with jax.named_scope("w_end"):
         pl.when(has_up)(cond_up.wait_send)
         pl.when(has_down)(cond_down.wait_send)
@@ -563,6 +588,21 @@
         drain(att_out.at[:, : n - 1], send.at[4])
         pl.when(has_up)(lambda: drain(act_out.at[0], send.at[5]))
         pl.when(has_down)(lambda: drain(act_out.at[1], send.at[6]))
+
+
+def add_up(main, tail, sums, att, out_hbm, out, sem):
+    frames_dev, rows, cols, channels = out.shape
+    per_row = sums.shape[2]
+    stores = []
+    for f in range(frames_dev):
+        for r in range(rows):
+            convolved = conv_row(sums[f, r].reshape(cols, -1), main, tail)
+            held = att[f, r * per_row : (r + 1) * per_row].astype(F32).reshape(cols, channels)
+            out[f, r] = (held + convolved).astype(BF16)
+        stores.append(pltpu.make_async_copy(out.at[f], out_hbm.at[f], sem.at[f]))
+        stores[f].start()
+    for store in stores:
+        store.wait()
 
 
 def shards(
@@ -620,11 +660,14 @@
         block_conv,
     ]
     values = [pltpu.with_memory_space_constraint(v, pltpu.MemorySpace.HBM) for v in values]
-    return pl.pallas_call(
+    sums_shape = pltpu.VMEM((frames_dev, rows, per_row, pieces, group, wide), F32)
+    att_shape = pltpu.VMEM((frames_dev, n, pieces, group, channels), BF16)
+    vmem = pl.BlockSpec(memory_space=pltpu.VMEM)
+    sums, att = pl.pallas_call(
         functools.partial(kernel, n, row_total),
-        out_shape=pltpu.VMEM(latents.shape, BF16),
+        out_shape=(sums_shape, att_shape),
         in_specs=[pl.BlockSpec(memory_space=pl.ANY)] * len(values),
-        out_specs=pl.BlockSpec(memory_space=pltpu.VMEM),
+        out_specs=(vmem, vmem),
         scratch_shapes=[
             pltpu.SMEM(key_frames.shape, jnp.int32),
             pltpu.SMEM(propagate.shape, jnp.int32),
@@ -634,16 +677,13 @@
             pltpu.VMEM(condition.shape, BF16),
             pltpu.VMEM((3, channels, wide), BF16),
             pltpu.VMEM((9, channels, tail), BF16),
-            pltpu.VMEM(square, BF16),
-            pltpu.VMEM(square, BF16),
-            pltpu.VMEM(square, BF16),
-            pltpu.VMEM(square, BF16),
-            pltpu.VMEM(square, BF16),
+            pltpu.VMEM((5,) + square, BF16),
             pltpu.VMEM((3, channels, wide), BF16),
             pltpu.VMEM((9, channels, tail), BF16),
             pltpu.VMEM(square, BF16),
             pltpu.VMEM((channels, 64 * HEADS), BF16),
             pltpu.VMEM((channels, 64 * HEADS), BF16),
+            pltpu.VMEM((2, block, channels), BF16),
             pltpu.VMEM((2, HEADS // 2, 2 * block, 128), BF16),
             pltpu.VMEM((2, block, 64 * HEADS), BF16),
             pltpu.VMEM((2, channels, block), BF16),
@@ -658,7 +698,6 @@
             pltpu.VMEM((frames, pix, channels), F32),
             pltpu.VMEM((pieces, n, att_size, group, 128), BF16),
             pltpu.VMEM((n, pieces, att_size, group, 128), BF16),
-            pltpu.VMEM((frames_dev, n, pieces, group, channels), BF16),
             pltpu.VMEM((frames_dev, rows, per_row, pieces, group, channels), BF16),
             pltpu.VMEM((2, slots, cond_size, 128), BF16),
             pltpu.VMEM((slots, cond_size, 128), BF16),
@@ -667,19 +706,26 @@
             pltpu.VMEM((pieces, frames_dev, act_size, 128), BF16),
             pltpu.VMEM((pieces, frames_dev, act_size, 128), BF16),
             pltpu.VMEM((slots, rows, cols, wide), F32),
-            pltpu.VMEM((frames_dev, rows, per_row, pieces, group, wide), F32),
-            dma((16,)),
+            dma((12,)),
             dma((7,)),
             dma((1,)),
             dma((chunks,)),
             dma((pieces,)),
             dma((2,)),
-            dma((2, pieces)),
+            dma((2, 2)),
         ],
         compiler_params=pltpu.CompilerParams(
             collective_id=0, has_side_effects=True, vmem_limit_bytes=48 * 1024 * 1024
         ),
     )(*values)
+    return pl.pallas_call(
+        functools.partial(add_up, main, tail),
+        out_shape=jax.ShapeDtypeStruct(latents.shape, BF16),
+        in_specs=[vmem, vmem],
+        out_specs=pl.BlockSpec(memory_space=pl.ANY),
+        scratch_shapes=[pltpu.VMEM(latents.shape, BF16), dma((frames_dev,))],
+        compiler_params=pltpu.CompilerParams(vmem_limit_bytes=4 * 1024 * 1024),
+    )(sums, att)
 
 
 def solution(mesh):

time: 28.4 us -> 27.7 us (0.975)
  local copies, waits for them, and re-layouts: 0.82 us -> 0 us
    unnamed x1 -> x0, local copies, waits for them, and re-layouts: 0.82 us -> none
    pallas_call x1 -> x2, Pallas kernels: 27.4 us -> 27.5 us  [the longest x1 26.4 us: shards(): pl.pallas_call(functools.partial(kernel, n, row_total), out_shape=(sums_s...]
where the time goes in v2:
time: 27.7 us; the launch traced here: 27.6 us
  Pallas kernels  27.5 us (99%)
    pallas_call x1, Pallas kernels, shards(): pl.pallas_call(functools.partial(kernel, n, row_total), out_shape=(sums_s...  26.4 us
    pallas_call x1, Pallas kernels, shards(): pl.pallas_call(functools.partial(add_up, main, tail), out_shape=jax.Shape...  1.1 us

profile of v2, /device:TPU:0, one launch (start us, length us, event | category | flops | bytes accessed | tf_op | source)
XLA Modules:
  0.0 27.6 jit_solution(15828529472307031932)
XLA Ops:
  0.0 26.4 %shard_map.136 = (f32[6,2,2,4,8,960]{5,4,3,2,1,0:T(8,128)S(1)}, bf16[6,4,4,8,320]{4,3,2,1,0:T(8,128)(2,1)S(1)}) custom-call(bf16[6,4,32,320]{3,2,1,0:T(8,128)(2,1)} %bitcast.1, bf16[3,2,64,320]{3,2,1,0:T(8,128)(2,1)} %cond_hbm.1, s32[12]{0:T(128)} %key_hbm.1, s32[24]{0:T(128)} %prop_hbm.1, f32[24,320]{1,0:T(8,128)} %constant.2.clone.encoding_hbm, ...), custom_call_target="tpu_custom_call" | custom-call | tf_op jit(solution)/shard_map/pallas_call | solution.py:666
  26.5 1.1 %shard_map.137 = bf16[6,2,64,320]{3,2,1,0:T(8,128)(2,1)} custom-call(f32[6,2,2,4,8,960]{5,4,3,2,1,0:T(8,128)S(1)} %get-tuple-element.7.sums, bf16[6,4,4,8,320]{4,3,2,1,0:T(8,128)(2,1)S(1)} %get-tuple-element.8.att), custom_call_target="tpu_custom_call" | custom-call | tf_op jit(solution)/shard_map/pallas_call | solution.py:721

commit v3 on v2

--- a/solution.py
+++ b/solution.py
@@ -211,12 +211,16 @@
     chunks = res_recv.shape[0]
     chunk = pix // chunks
     frames = hidden.shape[0]
-    pieces, group = att.shape[2:4]
+    pieces, group = att.shape[3:5]
     per_chunk = chunk // group
     per_row = n // rows
     head_dim = channels // HEADS
     main = enc_w.shape[2] // 3 // 128 * 128
     tail = channels - main
+    def block_of(p):
+        return p % rows * per_row + p // rows
+
+    home = lax.div(me, rows)
     has_up = row_me > 0
     has_down = row_me < row_total - 1
 
@@ -305,7 +309,7 @@
 
     loads[1].wait()
     for p in range(n):
-        lat_out[p] = pack_rows(lat_own[:, p].astype(F32)).astype(BF16)
+        lat_out[p] = pack_rows(lat_own[:, block_of(p)].astype(F32)).astype(BF16)
     peers = [lax.rem(me + k, n) for k in range(1, n)]
     for peer in peers:
         remote(
@@ -361,7 +365,7 @@
         keyres = dot(encoded, squares[1]).reshape(slots, n, pix, channels)
         for p in range(n):
             for c in range(chunks):
-                part = pack_rows(keyres[:, p, c * chunk : (c + 1) * chunk])
+                part = pack_rows(keyres[:, block_of(p), c * chunk : (c + 1) * chunk])
                 res_out[p, c] = part.astype(BF16)
     for c in range(chunks):
         for peer in peers:
@@ -470,28 +474,47 @@
                 att_out.at[s, peer],
                 att_in.at[me, s],
                 send.at[4],
-                att_recv.at[s],
+                att_recv.at[s, (lax.div(peer, rows) != home).astype(jnp.int32)],
                 frame=peer,
             ).start()
         att_in[me, s] = att_out[s, me]
 
-    def activate(s):
-        with jax.named_scope(f"w_att{s}"):
-            drain(att_in.at[: n - 1, s], att_recv.at[s])
-        with jax.named_scope(f"act{s}"):
-            taken = [unpack_lead(att_in[p, s].astype(F32), frames_dev, channels) for p in range(n)]
-            value = jnp.stack(taken, axis=1)
-            att[:, :, s] = value.astype(BF16)
-            value = silu(norm(value, gain_c[...])).reshape(frames_dev, rows, -1, channels)
-            act_out[0, s] = pack_rows(value[:, 0]).astype(BF16)
-            act_out[1, s] = pack_rows(value[:, rows - 1]).astype(BF16)
-            value = value.reshape(frames_dev, rows, per_row, group, channels)
-            act[:, :, :, s] = value.astype(BF16)
+    def activate_block(s, block):
+        taken = [
+            unpack_lead(att_in[block * rows + r, s].astype(F32), frames_dev, channels)
+            for r in range(rows)
+        ]
+        value = jnp.stack(taken, axis=1)
+        active = silu(norm(value, gain_c[...]))
+        act_out[0, s, block] = pack_lead(active[:, 0]).astype(BF16)
+        act_out[1, s, block] = pack_lead(active[:, rows - 1]).astype(BF16)
         which = 1 if s == pieces - 1 else 0
-        act_up = up(act_out.at[0, s], act_bot.at[s], send.at[5], ah_recv.at[0, which])
-        act_down = down(act_out.at[1, s], act_top.at[s], send.at[6], ah_recv.at[1, which])
+        act_up = up(
+            act_out.at[0, s, block], act_bot.at[s, block], send.at[5], ah_recv.at[0, which]
+        )
+        act_down = down(
+            act_out.at[1, s, block], act_top.at[s, block], send.at[6], ah_recv.at[1, which]
+        )
         pl.when(has_up)(act_up.start)
         pl.when(has_down)(act_down.start)
+        att[:, :, block, s] = value.astype(BF16)
+        act[:, :, block, s] = active.astype(BF16)
+
+    def activate_home(s):
+        if rows > 1:
+            drain(att_in.at[: rows - 1, s], att_recv.at[s, 0])
+        activate_block(s, home)
+
+    def activate_rest(s):
+        drain(att_in.at[: n - rows, s], att_recv.at[s, 1])
+        for i in range(1, per_row):
+            activate_block(s, lax.rem(home + i, per_row))
+
+    def activate(s):
+        with jax.named_scope(f"home{s}"):
+            activate_home(s)
+        with jax.named_scope(f"rest{s}"):
+            activate_rest(s)
 
     def attend_all():
         turns = [(s, j) for s in range(pieces) for j in range(pairs_total)]
@@ -553,7 +576,12 @@
                 finish(s)
 
     def add_b(r, span, ref, taps):
-        parts = [edge_rows(ref, (s,), per_row * group) for s in range(span.start, span.stop)]
+        parts = []
+        for s in range(span.start, span.stop):
+            taken = [
+                unpack_lead(ref[s, q].astype(F32), frames_dev, channels) for q in range(per_row)
+            ]
+            parts.append(jnp.stack(taken, axis=1).reshape(-1, channels).astype(BF16))
         value = dot(jnp.concatenate(parts, axis=0), taps)
         value = value.reshape(len(parts), frames_dev, per_row, group, value.shape[-1])
         for i, s in enumerate(range(span.start, span.stop)):
@@ -592,12 +620,11 @@
 
 def add_up(main, tail, sums, att, out_hbm, out, sem):
     frames_dev, rows, cols, channels = out.shape
-    per_row = sums.shape[2]
     stores = []
     for f in range(frames_dev):
         for r in range(rows):
             convolved = conv_row(sums[f, r].reshape(cols, -1), main, tail)
-            held = att[f, r * per_row : (r + 1) * per_row].astype(F32).reshape(cols, channels)
+            held = att[f, r].astype(F32).reshape(cols, channels)
             out[f, r] = (held + convolved).astype(BF16)
         stores.append(pltpu.make_async_copy(out.at[f], out_hbm.at[f], sem.at[f]))
         stores[f].start()
@@ -638,7 +665,6 @@
     lat_size = packed_size(pix, channels)
     res_size = packed_size(chunk, channels)
     cond_size = packed_size(cols, channels)
-    act_size = packed_size(per_row * group, channels)
     att_size = frames_dev * (channels // 128) + frames_dev // 2
     encoding = jnp.asarray(positions(frames, channels))
     square = (channels, channels)
@@ -661,7 +687,7 @@
     ]
     values = [pltpu.with_memory_space_constraint(v, pltpu.MemorySpace.HBM) for v in values]
     sums_shape = pltpu.VMEM((frames_dev, rows, per_row, pieces, group, wide), F32)
-    att_shape = pltpu.VMEM((frames_dev, n, pieces, group, channels), BF16)
+    att_shape = pltpu.VMEM((frames_dev, rows, per_row, pieces, group, channels), BF16)
     vmem = pl.BlockSpec(memory_space=pltpu.VMEM)
     sums, att = pl.pallas_call(
         functools.partial(kernel, n, row_total),
@@ -702,15 +728,15 @@
             pltpu.VMEM((2, slots, cond_size, 128), BF16),
             pltpu.VMEM((slots, cond_size, 128), BF16),
             pltpu.VMEM((slots, cond_size, 128), BF16),
-            pltpu.VMEM((2, pieces, frames_dev, act_size, 128), BF16),
-            pltpu.VMEM((pieces, frames_dev, act_size, 128), BF16),
-            pltpu.VMEM((pieces, frames_dev, act_size, 128), BF16),
+            pltpu.VMEM((2, pieces, per_row, att_size, group, 128), BF16),
+            pltpu.VMEM((pieces, per_row, att_size, group, 128), BF16),
+            pltpu.VMEM((pieces, per_row, att_size, group, 128), BF16),
             pltpu.VMEM((slots, rows, cols, wide), F32),
             dma((12,)),
             dma((7,)),
             dma((1,)),
             dma((chunks,)),
-            dma((pieces,)),
+            dma((pieces, 2)),
             dma((2,)),
             dma((2, 2)),
         ],

time: 27.7 us -> 27.5 us (level)
  no operation moved by 1% of the time
where the time goes in v3:
time: 27.5 us; the launch traced here: 27.3 us
  Pallas kernels  27.3 us (99%)
    pallas_call x1, Pallas kernels, shards(): pl.pallas_call(functools.partial(kernel, n, row_total), out_shape=(sums_s...  26.2 us
    pallas_call x1, Pallas kernels, shards(): pl.pallas_call(functools.partial(add_up, main, tail), out_shape=jax.Shape...  1.1 us

profile of v3, /device:TPU:0, one launch (start us, length us, event | category | flops | bytes accessed | tf_op | source)
XLA Modules:
  0.0 27.3 jit_solution(4986424190364987678)
XLA Ops:
  0.0 26.2 %shard_map.136 = (f32[6,2,2,4,8,960]{5,4,3,2,1,0:T(8,128)S(1)}, bf16[6,2,2,4,8,320]{5,4,3,2,1,0:T(8,128)(2,1)S(1)}) custom-call(bf16[6,4,32,320]{3,2,1,0:T(8,128)(2,1)} %bitcast.1, bf16[3,2,64,320]{3,2,1,0:T(8,128)(2,1)} %cond_hbm.1, s32[12]{0:T(128)} %key_hbm.1, s32[24]{0:T(128)} %prop_hbm.1, f32[24,320]{1,0:T(8,128)} %constant.2.clone.encoding_hbm, ...), custom_call_target="tpu_custom_call" | custom-call | tf_op jit(solution)/shard_map/pallas_call | solution.py:692
  26.2 1.1 %shard_map.137 = bf16[6,2,64,320]{3,2,1,0:T(8,128)(2,1)} custom-call(f32[6,2,2,4,8,960]{5,4,3,2,1,0:T(8,128)S(1)} %get-tuple-element.7.sums, bf16[6,2,2,4,8,320]{5,4,3,2,1,0:T(8,128)(2,1)S(1)} %get-tuple-element.8.att), custom_call_target="tpu_custom_call" | custom-call | tf_op jit(solution)/shard_map/pallas_call | solution.py:747

commit v4 on v3

--- a/solution.py
+++ b/solution.py
@@ -620,16 +620,13 @@
 
 def add_up(main, tail, sums, att, out_hbm, out, sem):
     frames_dev, rows, cols, channels = out.shape
-    stores = []
     for f in range(frames_dev):
         for r in range(rows):
             convolved = conv_row(sums[f, r].reshape(cols, -1), main, tail)
             held = att[f, r].astype(F32).reshape(cols, channels)
             out[f, r] = (held + convolved).astype(BF16)
-        stores.append(pltpu.make_async_copy(out.at[f], out_hbm.at[f], sem.at[f]))
-        stores[f].start()
-    for store in stores:
-        store.wait()
+            pltpu.make_async_copy(out.at[f, r], out_hbm.at[f, r], sem).start()
+    pltpu.make_async_copy(out, out_hbm, sem).wait()
 
 
 def shards(
@@ -749,7 +746,7 @@
         out_shape=jax.ShapeDtypeStruct(latents.shape, BF16),
         in_specs=[vmem, vmem],
         out_specs=pl.BlockSpec(memory_space=pl.ANY),
-        scratch_shapes=[pltpu.VMEM(latents.shape, BF16), dma((frames_dev,))],
+        scratch_shapes=[pltpu.VMEM(latents.shape, BF16), dma],
         compiler_params=pltpu.CompilerParams(vmem_limit_bytes=4 * 1024 * 1024),
     )(sums, att)
 

time: 27.5 us -> 27.4 us (level)
  no operation moved by 1% of the time
where the time goes in v4:
time: 27.4 us; the launch traced here: 27.2 us
  Pallas kernels  27.2 us (99%)
    pallas_call x1, Pallas kernels, shards(): pl.pallas_call(functools.partial(kernel, n, row_total), out_shape=(sums_s...  26.2 us
    pallas_call x1, Pallas kernels, shards(): pl.pallas_call(functools.partial(add_up, main, tail), out_shape=jax.Shape...  1.03 us

profile of v4, /device:TPU:0, one launch (start us, length us, event | category | flops | bytes accessed | tf_op | source)
XLA Modules:
  0.0 27.2 jit_solution(14024721649490708583)
XLA Ops:
  0.0 26.2 %shard_map.136 = (f32[6,2,2,4,8,960]{5,4,3,2,1,0:T(8,128)S(1)}, bf16[6,2,2,4,8,320]{5,4,3,2,1,0:T(8,128)(2,1)S(1)}) custom-call(bf16[6,4,32,320]{3,2,1,0:T(8,128)(2,1)} %bitcast.1, bf16[3,2,64,320]{3,2,1,0:T(8,128)(2,1)} %cond_hbm.1, s32[12]{0:T(128)} %key_hbm.1, s32[24]{0:T(128)} %prop_hbm.1, f32[24,320]{1,0:T(8,128)} %constant.2.clone.encoding_hbm, ...), custom_call_target="tpu_custom_call" | custom-call | tf_op jit(solution)/shard_map/pallas_call | solution.py:689
  26.2 1.0 %shard_map.137 = bf16[6,2,64,320]{3,2,1,0:T(8,128)(2,1)} custom-call(f32[6,2,2,4,8,960]{5,4,3,2,1,0:T(8,128)S(1)} %get-tuple-element.7.sums, bf16[6,2,2,4,8,320]{5,4,3,2,1,0:T(8,128)(2,1)S(1)} %get-tuple-element.8.att), custom_call_target="tpu_custom_call" | custom-call | tf_op jit(solution)/shard_map/pallas_call | solution.py:744
